TPU v7x, 128 devices: a whole 4x4x4 slice. The times are simulated.
128 devices in a mesh: dp: 32 (over x, y, z_hi), pipe: 4 (over z_lo, core).
Axes of the slice: x: 4, y: 4, z: 4 (z_hi: 2, z_lo: 2; z = z_hi * 2 + z_lo), core: 2. Of those that a mesh axis runs over, the one named last changes fastest.
Arguments:
- master: float32 [4, 512, 8192], P('pipe', 'dp'), may hold values from -0.12 to 0.12
- moment1: float32 [4, 512, 8192], P('pipe', 'dp'), may hold values from -3 to 3
- moment2: float32 [4, 512, 8192], P('pipe', 'dp'), may hold values from 0.25 to 4.5
- quant_grad: bfloat16 [4, 512, 8192], P('pipe', 'dp'), may hold values from -120 to 120
- grad_exponent: int32 [4, 512], P('pipe', 'dp'), may hold values from -3 to 2
- replica_params: bfloat16 [4, 32, 512, 8192], P('pipe', 'dp'), as said below
- failed: int32 [4, 2], replicated, may hold values from 0 to 31, as said below
- dest: int32 [4, 512], replicated, may hold values from 0 to 511, as said below
Outputs:
- new_master: float32 [4, 512, 8192], P('pipe', 'dp')
- new_moment1: float32 [4, 512, 8192], P('pipe', 'dp')
- new_moment2: float32 [4, 512, 8192], P('pipe', 'dp')
Inputs may be any that keep to these rules, and one draw needn't show every extreme that they name: `failed`: each group lists 2 distinct ranks; group 0 lists ranks 1 and 16; in every other group some rows of the first listed rank have new positions among the rows of the second listed rank (new position // 16). `dest`: each group's row is a permutation of its rows; the 16 rows of one rank (old rows r * 16 to r * 16 + 15) land in at most 1 row of any one rank's new rows (new position // 16), and some pair of ranks reaches 1 in every group. `replica_params`: within a group the copies of ranks not listed in failed are equal; the copies of listed ranks are zero.
All inputs are finite; a program needn't handle non-finite values.
Results may differ from a plain program's by a relative error of at most 0.0003.
Values may be sent and summed in bfloat16 or wider, within the bound.
A program may use at most 64 MiB of HBM per device.

v0:
```python
import jax
import jax.numpy as jnp
from jax import lax
from jax.sharding import PartitionSpec as P

STEP = 20
beta_one = 0.9
beta_two = 0.95
learn_rate = 0.00015
decay_rate = 0.1
adam_eps = 1e-08
clip_eps = 1e-06


def from_root(value, axis, source):
    kept = jnp.where(lax.axis_index(axis) == source, value, 0).astype(value.dtype)
    return lax.psum(kept, axis)


def adam_step(weights, first, second, grads):
    first_new = beta_one * first + (1.0 - beta_one) * grads
    second_new = beta_two * second + (1.0 - beta_two) * grads * grads
    corr_one = 1.0 - beta_one**STEP
    corr_two = 1.0 - beta_two**STEP
    direction = (
        first_new / corr_one / (jnp.sqrt(second_new / corr_two) + adam_eps) + decay_rate * weights
    )
    return (weights - learn_rate * direction, first_new, second_new)


def local(master, moment1, moment2, quant_grad, grad_exponent, replica_params, failed, dest):
    group_idx = lax.axis_index("pipe")
    my_rank = lax.axis_index("dp")
    ranks_count = lax.axis_size("dp")
    shard_rows = master.shape[1]
    row_width = master.shape[2]
    fail_count = failed.shape[1]
    peer_slots = (shard_rows + ranks_count - 1) // ranks_count
    fail_row = lax.dynamic_index_in_dim(failed, group_idx, 0, keepdims=False)
    dest_row = lax.dynamic_index_in_dim(dest, group_idx, 0, keepdims=False)
    rank_ids = jnp.arange(ranks_count, dtype=jnp.int32)
    is_alive = jnp.all(rank_ids[:, None] != fail_row[None, :], axis=1)
    own_fail = fail_row == my_rank
    is_lost = jnp.any(own_fail)
    copy_rows = replica_params[0, 0]
    first_root = jnp.min(jnp.where(is_alive, rank_ids, ranks_count))
    bf_zero = jnp.zeros((), jnp.bfloat16)
    local_ids = jnp.arange(shard_rows, dtype=jnp.int32)
    group_ids = jnp.arange(dest_row.shape[0], dtype=jnp.int32)
    targets = (dest_row // shard_rows).reshape(ranks_count, shard_rows)
    earlier = local_ids[None, :] < local_ids[:, None]
    same_target = targets[:, :, None] == targets[:, None, :]
    order_in = jnp.sum((same_target & earlier[None, :, :]).astype(jnp.int32), axis=2)
    my_targets = lax.dynamic_index_in_dim(targets, my_rank, 0, keepdims=False)
    my_order = lax.dynamic_index_in_dim(order_in, my_rank, 0, keepdims=False)
    slot_ids = jnp.arange(peer_slots, dtype=jnp.int32)
    pick_mask = (my_targets[None, None, :] == rank_ids[:, None, None]) & (
        my_order[None, None, :] == slot_ids[None, :, None]
    )
    send_index = jnp.sum(jnp.where(pick_mask, local_ids[None, None, :], 0), axis=2).reshape(-1)
    new_rows = my_rank * shard_rows + local_ids
    match_mask = dest_row[None, :] == new_rows[:, None]
    source_row = jnp.sum(jnp.where(match_mask, group_ids[None, :], 0), axis=1)
    source_rank = source_row // shard_rows
    source_order = order_in.reshape(-1)[source_row]
    recv_index = source_rank * peer_slots + source_order
    master_extra = None
    lost_blocks = jnp.stack(
        [
            lax.dynamic_slice_in_dim(copy_rows, fail_row[piece_idx] * shard_rows, shard_rows, 0)
            for piece_idx in range(fail_count)
        ]
    )
    lost_blocks = jnp.where(my_rank == first_root, lost_blocks, bf_zero)
    received_rows = from_root(lost_blocks, "dp", first_root)
    recovered = jnp.sum(
        jnp.where(own_fail[:, None, None], received_rows.astype(jnp.float32), jnp.float32(0.0)),
        axis=0,
    )
    start_master = jnp.where(is_lost, recovered, master[0])
    start_first = jnp.where(is_lost, jnp.float32(0.0), moment1[0])
    start_second = jnp.where(is_lost, jnp.float32(0.0), moment2[0])
    grad = (
        quant_grad[0].astype(jnp.float32) * jnp.exp2(grad_exponent[0].astype(jnp.float32))[:, None]
    )
    grad_total = lax.psum(jnp.sum(grad * grad), ("dp", "pipe"))
    elem_count = lax.axis_size("dp") * lax.axis_size("pipe") * shard_rows * row_width
    clip_scale = jnp.minimum(1.0, 1.0 / jnp.sqrt(grad_total / elem_count + clip_eps))
    clipped = grad * clip_scale

    def to_buffer(values):
        return values[send_index].reshape(ranks_count, peer_slots, row_width)

    w_next, m_next, v_next = adam_step(start_master, start_first, start_second, clipped)
    received = (
        lax.all_to_all(to_buffer(w_next), "dp", split_axis=0, concat_axis=0, tiled=True),
        lax.all_to_all(to_buffer(m_next), "dp", split_axis=0, concat_axis=0, tiled=True),
        lax.all_to_all(to_buffer(v_next), "dp", split_axis=0, concat_axis=0, tiled=True),
    )
    placed = tuple(
        (values.reshape(ranks_count * peer_slots, row_width)[recv_index] for values in received)
    )
    placed_master = placed[0]
    return (placed_master[None], placed[1][None], placed[2][None])


def solution(mesh):
    in_specs = (
        P("pipe", "dp", None),
        P("pipe", "dp", None),
        P("pipe", "dp", None),
        P("pipe", "dp", None),
        P("pipe", "dp"),
        P("pipe", "dp", None, None),
        P(),
        P(),
    )
    out_specs = (P("pipe", "dp", None), P("pipe", "dp", None), P("pipe", "dp", None))
    return jax.shard_map(local, mesh=mesh, in_specs=in_specs, out_specs=out_specs, check_vma=False)
```

profile of v0, /device:TPU:0, one launch (start us, length us, event | category | flops | bytes accessed | tf_op | source)
XLA Modules:
  0.0 445.7 jit_solution(17643683241588214400)
XLA Ops:
  7.2 0.9 fusion.19
  8.1 0.5 fusion.20
  10.0 0.6 select_reduce_fusion.3
  11.3 1.1 dynamic-slice_bitcast_fusion.1
  12.4 0.9 fusion.1
  13.3 0.7 exponential_bitcast_fusion
  13.9 1.8 fusion.6
  15.7 69.2 %psum.15 = f32[]{:T(128)} all-reduce(f32[]{:T(128)} %fusion.6), channel_id=1, replica_groups=mesh['dp'=32,'pipe'=4] {'dp','pipe'}, use_global_device_ids=true, to_apply=%region_6.7 | all-reduce | flops 1 | bytes 8 | tf_op jit(solution)/shard_map/psum | solution.py:86
  86.1 1.4 fusion.15
  88.0 0.6 fusion.18
  88.7 277.0 %all-reduce.2.cloned.1.call-done = bf16[2,16,8192]{2,1,0:T(8,128)(2,1)} async-done(((bf16[2,16,8192]{2,1,0:T(8,128)(2,1)}), bf16[2,16,8192]{2,1,0:T(8,128)(2,1)}) %all-reduce.2.cloned.1.call-update) | async-done | bytes 524304 | tf_op jit(solution)/shard_map/psum | solution.py:17
  365.7 1.3 select_reduce_fusion
  367.0 2.7 multiply_subtract_fusion
  369.7 0.9 gather_fusion
  370.6 2.1 copy.22
  372.7 10.0 %all-to-all-start = ((f32[32,1,8192]{2,1,0:T(1,128)}), f32[32,1,8192]{2,1,0:T(1,128)S(1)}, u32[]{:S(2)}, u32[]{:S(2)}) async-start(f32[32,1,8192]{2,1,0:T(1,128)} %copy.22), calls=%async_computation | async-start | bytes 2097152 | tf_op jit(solution)/shard_map/all_to_all | solution.py:96
  382.7 0.9 gather_fusion.3
  383.6 2.1 copy.24
  385.7 12.2 %all-to-all-done = f32[32,1,8192]{2,1,0:T(1,128)S(1)} async-done(((f32[32,1,8192]{2,1,0:T(1,128)}), f32[32,1,8192]{2,1,0:T(1,128)S(1)}, u32[]{:S(2)}, u32[]{:S(2)}) %all-to-all-start) | async-done | bytes 1048608 | tf_op jit(solution)/shard_map/all_to_all | solution.py:96
  397.8 4.7 %all-to-all-start.1 = ((f32[32,1,8192]{2,1,0:T(1,128)}), f32[32,1,8192]{2,1,0:T(1,128)}, u32[]{:S(2)}, u32[]{:S(2)}) async-start(f32[32,1,8192]{2,1,0:T(1,128)} %copy.24), calls=%async_computation.1 | async-start | bytes 2097152 | tf_op jit(solution)/shard_map/all_to_all | solution.py:97
  402.5 0.9 gather_fusion.5
  403.4 2.1 copy.25
  405.5 12.5 %all-to-all-done.1 = f32[32,1,8192]{2,1,0:T(1,128)} async-done(((f32[32,1,8192]{2,1,0:T(1,128)}), f32[32,1,8192]{2,1,0:T(1,128)}, u32[]{:S(2)}, u32[]{:S(2)}) %all-to-all-start.1) | async-done | bytes 1048608 | tf_op jit(solution)/shard_map/all_to_all | solution.py:97
  418.0 3.9 all-to-all-start.2
  422.3 0.7 gather_fusion.1
  423.0 0.6 copy.34
  423.6 1.5 gather_fusion.2
  425.1 1.8 copy.33
  426.9 1.5 gather_fusion.4
  428.4 8.3 %all-to-all-done.2 = f32[32,1,8192]{2,1,0:T(1,128)S(1)} async-done(((f32[32,1,8192]{2,1,0:T(1,128)}), f32[32,1,8192]{2,1,0:T(1,128)S(1)}, u32[]{:S(2)}, u32[]{:S(2)}) %all-to-all-start.2) | async-done | bytes 1048608 | tf_op jit(solution)/shard_map/all_to_all | solution.py:98
  436.7 0.6 copy.32
  437.3 1.5 gather_fusion.6
  (22 shorter events, 1.6 us)
Async XLA Ops:
  7.2 358.5 %all-reduce.2.cloned.1.call-start = ((), (), s32[]{:S(2)}) async-start(), calls=%async_computation.3 | async-start | bytes 1048576 | tf_op jit(solution)/shard_map/psum | solution.py:17
  372.7 25.1 %all-to-all-start = ((f32[32,1,8192]{2,1,0:T(1,128)}), f32[32,1,8192]{2,1,0:T(1,128)S(1)}, u32[]{:S(2)}, u32[]{:S(2)}) async-start(f32[32,1,8192]{2,1,0:T(1,128)} %copy.22), calls=%async_computation | async-start | bytes 2097152 | tf_op jit(solution)/shard_map/all_to_all | solution.py:96
  397.8 20.2 %all-to-all-start.1 = ((f32[32,1,8192]{2,1,0:T(1,128)}), f32[32,1,8192]{2,1,0:T(1,128)}, u32[]{:S(2)}, u32[]{:S(2)}) async-start(f32[32,1,8192]{2,1,0:T(1,128)} %copy.24), calls=%async_computation.1 | async-start | bytes 2097152 | tf_op jit(solution)/shard_map/all_to_all | solution.py:97
  418.0 18.7 %all-to-all-start.2 = ((f32[32,1,8192]{2,1,0:T(1,128)}), f32[32,1,8192]{2,1,0:T(1,128)S(1)}, u32[]{:S(2)}, u32[]{:S(2)}) async-start(f32[32,1,8192]{2,1,0:T(1,128)} %copy.25), calls=%async_computation.2 | async-start | bytes 2097152 | tf_op jit(solution)/shard_map/all_to_all | solution.py:98
Sparse Core Ops, SparseCore 0:
  13.4 352.2 all-reduce.1
where the time goes:
time: 446 us
  waiting for transfers between devices  310 us (70%)
  blocking collectives  69.2 us (16%)
  local copies, waits for them, and re-layouts  21.8 us (5%)
  starting transfers between devices  18.6 us (4%)
  between operations  16.8 us (4%)
  other arithmetic  9.3 us (2%)
    psum x1, waiting for transfers between devices, from_root(): return lax.psum(kept, axis)  277 us
    psum x1, blocking collectives, local(): grad_total = lax.psum(jnp.sum(grad * grad), ('dp', 'pipe'))  69.2 us
    all_to_all x1, waiting for transfers between devices, local(): lax.all_to_all(to_buffer(m_next), 'dp', split_axis=0, concat_axis=0, tile...  12.5 us
    all_to_all x1, waiting for transfers between devices, local(): lax.all_to_all(to_buffer(w_next), 'dp', split_axis=0, concat_axis=0, tile...  12.2 us
    all_to_all x1, starting transfers between devices, local(): lax.all_to_all(to_buffer(w_next), 'dp', split_axis=0, concat_axis=0, tile...  9.98 us
  transfers between devices with their start and end apart: 4, of which 4 were waited for; matrix products, arithmetic and copies ran while one was open for 4% of the time, Pallas kernels for 0%

commit v1 on v0

--- a/solution.py
+++ b/solution.py
@@ -12,9 +12,15 @@
 clip_eps = 1e-06
 
 
+def gather_and_add(x, axis):
+    terms = lax.all_gather(x, axis, axis=0, tiled=False)
+    total = terms.sum(axis=0)
+    return total
+
+
 def from_root(value, axis, source):
     kept = jnp.where(lax.axis_index(axis) == source, value, 0).astype(value.dtype)
-    return lax.psum(kept, axis)
+    return gather_and_add(kept, axis)
 
 
 def adam_step(weights, first, second, grads):

time: 446 us -> 265 us (0.59)
  waiting for transfers between devices: 310 us -> 122 us
  other arithmetic: 9.3 us -> 16.5 us
    psum x1 -> x0, waiting for transfers between devices: 277 us -> none  [from_root(): return lax.psum(kept, axis)]
    all_gather x0 -> x1, waiting for transfers between devices: none -> 81.1 us  [gather_and_add(): terms = lax.all_gather(x, axis, axis=0, tiled=False)]
    reduce_sum x0 -> x1, other arithmetic: none -> 8.72 us  [gather_and_add(): total = terms.sum(axis=0)]
    all_to_all x1, waiting for transfers between devices: 8.29 us -> 14.2 us  [local(): lax.all_to_all(to_buffer(v_next), 'dp', split_axis=0, concat_axis=0, tile...]
    all_to_all x1, starting transfers between devices: 9.98 us -> 4.11 us  [local(): lax.all_to_all(to_buffer(w_next), 'dp', split_axis=0, concat_axis=0, tile...]
  transfers between devices with their start and end apart: 4 -> 4, of which waited for: 4 -> 4; matrix products, arithmetic and copies ran while one was open for 4% -> 7% of each run, Pallas kernels for 0% -> 0%
where the time goes in v1:
time: 265 us; the launch traced here: 264 us
  waiting for transfers between devices  122 us (46%)
  blocking collectives  72.3 us (27%)
  local copies, waits for them, and re-layouts  21.8 us (8%)
  between operations  16.8 us (6%)
  other arithmetic  16.5 us (6%)
  starting transfers between devices  14.5 us (5%)
    all_gather x1, waiting for transfers between devices, gather_and_add(): terms = lax.all_gather(x, axis, axis=0, tiled=False)  81.1 us
    psum x1, blocking collectives, local(): grad_total = lax.psum(jnp.sum(grad * grad), ('dp', 'pipe'))  72.3 us
    all_to_all x1, waiting for transfers between devices, local(): lax.all_to_all(to_buffer(m_next), 'dp', split_axis=0, concat_axis=0, tile...  15.6 us
    all_to_all x1, waiting for transfers between devices, local(): lax.all_to_all(to_buffer(v_next), 'dp', split_axis=0, concat_axis=0, tile...  14.2 us
    all_to_all x1, waiting for transfers between devices, local(): lax.all_to_all(to_buffer(w_next), 'dp', split_axis=0, concat_axis=0, tile...  11.1 us
    reduce_sum x1, other arithmetic, gather_and_add(): total = terms.sum(axis=0)  8.72 us
    reshape x3, local copies, waits for them, and re-layouts, to_buffer(): return values[send_index].reshape(ranks_count, peer_slots, row_width)  6.25 us
    all_to_all x1, starting transfers between devices, local(): lax.all_to_all(to_buffer(m_next), 'dp', split_axis=0, concat_axis=0, tile...  5.72 us
  transfers between devices with their start and end apart: 4, of which 4 were waited for; matrix products, arithmetic and copies ran while one was open for 7% of the time, Pallas kernels for 0%

profile of v1, /device:TPU:0, one launch (start us, length us, event | category | flops | bytes accessed | tf_op | source)
XLA Modules:
  0.0 264.0 jit_solution(16288167504997490529)
XLA Ops:
  7.2 0.9 fusion.19
  8.1 0.5 fusion.20
  10.0 0.6 select_reduce_fusion.3
  11.3 1.1 constant_dynamic-slice_fusion.3
  12.4 0.9 fusion.1
  13.2 0.7 exponential_bitcast_fusion
  13.9 1.8 fusion.6
  15.7 72.3 %psum.7 = f32[]{:T(128)} all-reduce(f32[]{:T(128)} %fusion.6), channel_id=1, replica_groups=mesh['dp'=32,'pipe'=4] {'dp','pipe'}, use_global_device_ids=true, to_apply=%region_6.7 | all-reduce | flops 1 | bytes 8 | tf_op jit(solution)/shard_map/psum | solution.py:92
  89.2 1.4 fusion.15
  91.1 0.6 fusion.18
  91.8 81.1 %all-gather.2.cloned.1.call-done = bf16[32,2,16,8192]{3,2,1,0:T(8,128)(2,1)} async-done(((bf16[1,2,16,8192]{3,2,1,0:T(8,128)(2,1)}), bf16[32,2,16,8192]{3,2,1,0:T(8,128)(2,1)}) %all-gather.2.cloned.1.call-update) | async-done | bytes 16777232 | tf_op jit(solution)/shard_map/all_gather | solution.py:16
  172.9 8.7 %reduce_sum.61 = bf16[2,16,8192]{2,1,0:T(8,128)(2,1)S(1)} reduce(bf16[32,2,16,8192]{3,2,1,0:T(8,128)(2,1)} %all-gather.2.cloned.1.call-done, bf16[]{:T(256)} %constant.86.clone.1), dimensions={0}, to_apply=%region_3.4 | reduce | flops 8126464 | bytes 17301506 | tf_op jit(solution)/shard_map/reduce_sum | solution.py:17
  181.9 2.3 multiply_subtract_fusion
  184.2 0.9 gather_fusion.3
  185.1 2.1 copy.24
  187.2 5.7 %all-to-all-start.1 = ((f32[32,1,8192]{2,1,0:T(1,128)}), f32[32,1,8192]{2,1,0:T(1,128)S(1)}, u32[]{:S(2)}, u32[]{:S(2)}) async-start(f32[32,1,8192]{2,1,0:T(1,128)} %copy.24), calls=%async_computation.1 | async-start | bytes 2097152 | tf_op jit(solution)/shard_map/all_to_all | solution.py:103
  192.9 0.9 gather_fusion.5
  193.8 2.1 copy.25
  195.9 15.6 %all-to-all-done.1 = f32[32,1,8192]{2,1,0:T(1,128)S(1)} async-done(((f32[32,1,8192]{2,1,0:T(1,128)}), f32[32,1,8192]{2,1,0:T(1,128)S(1)}, u32[]{:S(2)}, u32[]{:S(2)}) %all-to-all-start.1) | async-done | bytes 1048608 | tf_op jit(solution)/shard_map/all_to_all | solution.py:103
  211.5 4.7 %all-to-all-start.2 = ((f32[32,1,8192]{2,1,0:T(1,128)}), f32[32,1,8192]{2,1,0:T(1,128)}, u32[]{:S(2)}, u32[]{:S(2)}) async-start(f32[32,1,8192]{2,1,0:T(1,128)} %copy.25), calls=%async_computation.2 | async-start | bytes 2097152 | tf_op jit(solution)/shard_map/all_to_all | solution.py:104
  216.2 0.9 gather_fusion
  217.1 2.1 copy.22
  219.2 14.2 %all-to-all-done.2 = f32[32,1,8192]{2,1,0:T(1,128)} async-done(((f32[32,1,8192]{2,1,0:T(1,128)}), f32[32,1,8192]{2,1,0:T(1,128)}, u32[]{:S(2)}, u32[]{:S(2)}) %all-to-all-start.2) | async-done | bytes 1048608 | tf_op jit(solution)/shard_map/all_to_all | solution.py:104
  233.4 4.1 %all-to-all-start = ((f32[32,1,8192]{2,1,0:T(1,128)}), f32[32,1,8192]{2,1,0:T(1,128)S(1)}, u32[]{:S(2)}, u32[]{:S(2)}) async-start(f32[32,1,8192]{2,1,0:T(1,128)} %copy.22), calls=%async_computation | async-start | bytes 2097152 | tf_op jit(solution)/shard_map/all_to_all | solution.py:102
  237.9 0.7 gather_fusion.1
  238.6 0.6 copy.33
  239.2 1.5 gather_fusion.4
  240.7 1.8 copy.32
  242.5 1.5 gather_fusion.6
  244.0 11.1 %all-to-all-done = f32[32,1,8192]{2,1,0:T(1,128)S(1)} async-done(((f32[32,1,8192]{2,1,0:T(1,128)}), f32[32,1,8192]{2,1,0:T(1,128)S(1)}, u32[]{:S(2)}, u32[]{:S(2)}) %all-to-all-start) | async-done | bytes 1048608 | tf_op jit(solution)/shard_map/all_to_all | solution.py:102
  255.1 0.6 copy.34
  255.7 1.5 gather_fusion.2
  (29 shorter events, 1.9 us)
Async XLA Ops:
  7.2 165.8 %all-gather.2.cloned.1.call-start = ((), (), s32[]{:S(2)}) async-start(), calls=%async_computation.3 | async-start | bytes 17301504 | tf_op jit(solution)/shard_map/all_gather | solution.py:16
  91.8 90.1 %copy-start = (bf16[1,16,8192]{2,1,0:T(8,128)(2,1)S(1)}, bf16[1,16,8192]{2,1,0:T(8,128)(2,1)}, u32[]{:S(2)}) copy-start(bf16[1,16,8192]{2,1,0:T(8,128)(2,1)} %param.11) | copy-start | bytes 786436
  91.8 90.1 %copy-start.1 = (f32[1,16,8192]{2,1,0:T(8,128)S(1)}, f32[1,16,8192]{2,1,0:T(8,128)}, u32[]{:S(2)}) copy-start(f32[1,16,8192]{2,1,0:T(8,128)} %param.8) | copy-start | bytes 1572868
  91.8 90.1 %copy-start.2 = (f32[1,16,8192]{2,1,0:T(8,128)S(1)}, f32[1,16,8192]{2,1,0:T(8,128)}, u32[]{:S(2)}) copy-start(f32[1,16,8192]{2,1,0:T(8,128)} %param.9) | copy-start | bytes 1572868
  187.2 24.4 %all-to-all-start.1 = ((f32[32,1,8192]{2,1,0:T(1,128)}), f32[32,1,8192]{2,1,0:T(1,128)S(1)}, u32[]{:S(2)}, u32[]{:S(2)}) async-start(f32[32,1,8192]{2,1,0:T(1,128)} %copy.24), calls=%async_computation.1 | async-start | bytes 2097152 | tf_op jit(solution)/shard_map/all_to_all | solution.py:103
  211.5 21.9 %all-to-all-start.2 = ((f32[32,1,8192]{2,1,0:T(1,128)}), f32[32,1,8192]{2,1,0:T(1,128)}, u32[]{:S(2)}, u32[]{:S(2)}) async-start(f32[32,1,8192]{2,1,0:T(1,128)} %copy.25), calls=%async_computation.2 | async-start | bytes 2097152 | tf_op jit(solution)/shard_map/all_to_all | solution.py:104
  233.4 21.7 %all-to-all-start = ((f32[32,1,8192]{2,1,0:T(1,128)}), f32[32,1,8192]{2,1,0:T(1,128)S(1)}, u32[]{:S(2)}, u32[]{:S(2)}) async-start(f32[32,1,8192]{2,1,0:T(1,128)} %copy.22), calls=%async_computation | async-start | bytes 2097152 | tf_op jit(solution)/shard_map/all_to_all | solution.py:102
Sparse Core Ops, SparseCore 0:
  13.4 159.5 all-gather.1
